TPU v7x, 32 devices: a whole 2x2x4 slice. The times are simulated.
32 devices in a mesh: ea: 8 (over z, x), sa: 4 (over y, core).
Axes of the slice: x: 2, y: 2, z: 4, core: 2. Of those that a mesh axis runs over, the one named last changes fastest.
Arguments:
- expert_hidden: bfloat16 [32, 1792, 512], P('ea', 'sa'), may hold values from -6 to 6
- down_weight: bfloat16 [32, 512, 2048], P('ea'), may hold values from -0.25 to 0.25
- residual: bfloat16 [8, 512, 2048], P('ea', 'sa'), may hold values from -6 to 6
- expert_ids: int32 [8, 512, 10], P('ea', 'sa'), may hold values from 0 to 31, all different within a row; in each aligned block of 128 rows (0 to 127, 128 to 255, ..., all dimensions but the last counted through in order) at most 56 rows name the same one
- combine_weight: float32 [8, 512, 10], P('ea', 'sa'), may hold values from 0.05 to 0.3
- norm_gain: bfloat16 [2048], replicated, may hold values from 0.25 to 1.75
- value_weight: bfloat16 [2048, 2048], P('ea'), may hold values from -0.125 to 0.125
- queries: bfloat16 [8, 512, 1024], P('ea', 'sa'), may hold values from -6 to 6
- keys: bfloat16 [8, 512, 1024], P('ea', 'sa'), may hold values from -6 to 6
- log_decay: float32 [8, 512, 16], P('ea', 'sa'), may hold values from -1 to 0, as said below
- write_rate: float32 [8, 512, 16], P('ea', 'sa'), may hold values from 0.1 to 0.9
Outputs:
- head_out: bfloat16 [8, 512, 2048], P('ea', 'sa')
Inputs may be any that keep to these rules, and one draw needn't show every extreme that they name: `expert_ids`: each row names 10 different experts; among the rows of one device (aligned blocks of 128 rows) no expert is named more than 56 times, a bound that some block reaches. `log_decay`: below zero.
All inputs are finite; a program needn't handle non-finite values.
Results may differ from a plain program's by a relative error of at most 0.0066.
Values may be sent and summed in bfloat16 or wider, within the bound.
A program may use at most 128 MiB of HBM per device.

v0:
```python
import jax
import jax.numpy as jnp
from jax import lax
from jax.sharding import PartitionSpec as P

HV = 16
HK = 8
DK = 128
DV = 128
SPAN = 64


PRECISION_LEVEL = lax.Precision.HIGHEST


def carried_in(shard, axis, combine, identity):
    count, here = (lax.axis_size(axis), lax.axis_index(axis))
    everything = jax.tree.map(lambda part: lax.all_gather(part, axis), shard)
    start = jax.tree.map(
        lambda part, zero: jnp.broadcast_to(jnp.asarray(zero, part.dtype), part.shape),
        shard,
        identity,
    )

    def turn(k, before):
        reached = k < here
        new = combine(before, jax.tree.map(lambda part: part[k], everything))
        return jax.tree.map(lambda a, b: jnp.where(reached, a, b), new, before)

    return lax.fori_loop(0, count, turn, start)


def unit_rows(field):
    return field * lax.rsqrt(jnp.sum(field * field, axis=-1, keepdims=True) + 1e-06)


def compose(earlier, later):
    first = jnp.einsum("hij,hjk->hik", later[0], earlier[0], precision=PRECISION_LEVEL)
    second = jnp.einsum("hij,hjk->hik", later[0], earlier[1], precision=PRECISION_LEVEL) + later[1]
    return (first, second)


def on_device(
    expert_hidden,
    down_weight,
    residual,
    expert_ids,
    combine_weight,
    norm_gain,
    value_weight,
    queries,
    keys,
    log_decay,
    write_rate,
):
    n_ea = lax.axis_size("ea")
    exp_dev, ff_units, width = down_weight.shape
    cap = expert_hidden.shape[1] // n_ea
    experts = exp_dev * n_ea
    tokens = residual.shape[1]
    top = expert_ids.shape[2]
    produced = jnp.einsum(
        "erf,efd->erd", expert_hidden, down_weight, preferred_element_type=jnp.float32
    )
    produced = produced.astype(jnp.bfloat16).reshape(exp_dev, n_ea, cap, width)
    ids = expert_ids[0]
    onehot = (ids[:, :, None] == jnp.arange(experts, dtype=jnp.int32)[None, None, :]).astype(
        jnp.float32
    )
    counts = jnp.sum(onehot, axis=1)
    earlier_rows = (
        lax.broadcasted_iota(jnp.int32, (tokens, tokens), 0)
        > lax.broadcasted_iota(jnp.int32, (tokens, tokens), 1)
    ).astype(jnp.float32)
    prior = jnp.dot(earlier_rows, counts, precision=PRECISION_LEVEL)
    slots = jnp.sum(onehot * prior[:, None, :], axis=-1).astype(jnp.int32)
    rows = (ids * cap + slots).reshape(tokens * top)
    weights = combine_weight[0]

    def combine(received):
        flat = received.reshape(experts * cap, -1)
        picked = jnp.take(flat, rows, axis=0).reshape(tokens, top, flat.shape[1])
        return jnp.sum(weights[:, :, None] * picked.astype(jnp.float32), axis=1)

    moe = combine(lax.all_to_all(produced, "ea", split_axis=1, concat_axis=0, tiled=True))
    stream = (residual[0].astype(jnp.float32) + moe).astype(jnp.bfloat16)
    flow_float32 = lax.optimization_barrier(stream).astype(jnp.float32)
    normed = (
        flow_float32
        * lax.rsqrt(jnp.mean(flow_float32 * flow_float32, axis=-1, keepdims=True) + 1e-06)
        * norm_gain.astype(jnp.float32)
    )
    normed = normed.astype(jnp.bfloat16)
    values = jnp.dot(
        normed,
        lax.all_gather(value_weight, "ea", axis=0, tiled=True),
        preferred_element_type=jnp.float32,
    ).astype(jnp.bfloat16)
    values = lax.optimization_barrier(values).astype(jnp.float32)
    blocks = tokens // SPAN

    def heads_first(field):
        return field.reshape(blocks, SPAN, HV, -1).transpose(0, 2, 1, 3)

    qn = unit_rows(queries[0].astype(jnp.float32).reshape(tokens, HK, DK)) * DK ** (-0.5)
    kn = unit_rows(keys[0].astype(jnp.float32).reshape(tokens, HK, DK))
    qh = heads_first(jnp.repeat(qn, HV // HK, axis=1))
    kh = heads_first(jnp.repeat(kn, HV // HK, axis=1))
    vh = heads_first(values.reshape(tokens, HV, DV))
    decay = log_decay[0].reshape(blocks, SPAN, HV).transpose(0, 2, 1)
    rate = write_rate[0].reshape(blocks, SPAN, HV).transpose(0, 2, 1)
    summed = jnp.cumsum(decay, axis=-1)
    row_pos = lax.broadcasted_iota(jnp.int32, (SPAN, SPAN), 0)
    col_pos = lax.broadcasted_iota(jnp.int32, (SPAN, SPAN), 1)
    inclusive = row_pos >= col_pos
    strict_lower = row_pos > col_pos
    diff = summed[..., :, None] - summed[..., None, :]
    ratio = jnp.where(inclusive, jnp.exp(jnp.where(inclusive, diff, 0.0)), 0.0)
    intersections = jnp.einsum("nhtk,nhjk->nhtj", kh, kh, precision=PRECISION_LEVEL)
    lower = jnp.where(strict_lower, rate[..., :, None] * ratio * intersections, 0.0)
    system = jnp.eye(SPAN, dtype=jnp.float32) + lower
    growth = jnp.exp(summed)
    rhs = jnp.concatenate([rate[..., None] * vh, (rate * growth)[..., None] * kh], axis=-1)
    solved = jax.scipy.linalg.solve_triangular(system, rhs, lower=True, unit_diagonal=True)
    delta_zero = solved[..., :DV]
    emat = solved[..., DV:]
    tail = jnp.exp(summed[..., -1:] - summed)
    ktail = kh * tail[..., None]
    amat = jnp.exp(summed[..., -1])[..., None, None] * jnp.eye(DK, dtype=jnp.float32) - jnp.einsum(
        "nhck,nhcj->nhkj", ktail, emat, precision=PRECISION_LEVEL
    )
    bmat = jnp.einsum("nhck,nhcv->nhkv", ktail, delta_zero, precision=PRECISION_LEVEL)
    scores = jnp.einsum("nhtk,nhjk->nhtj", qh, kh, precision=PRECISION_LEVEL) * ratio
    out_zero = jnp.einsum("nhtj,nhjv->nhtv", scores, delta_zero, precision=PRECISION_LEVEL)
    gmat = growth[..., None] * qh - jnp.einsum(
        "nhtj,nhjk->nhtk", scores, emat, precision=PRECISION_LEVEL
    )
    ident = jnp.broadcast_to(jnp.eye(DK, dtype=jnp.float32), (HV, DK, DK))
    nothing = jnp.zeros((HV, DK, DV), jnp.float32)

    def fold_block(carry, pair):
        return (compose(carry, pair), None)

    device_map, unused = lax.scan(fold_block, (ident, nothing), (amat, bmat))
    prefix = carried_in(device_map, "sa", compose, (ident, nothing))
    start_state = prefix[1]

    def emit_block(running_state, inputs):
        a_blk, b_blk, output_block, gate_block = inputs
        final_result = output_block + jnp.einsum(
            "yfw,ywp->yfp", gate_block, running_state, precision=PRECISION_LEVEL
        )
        running_state = (
            jnp.einsum("hij,hjv->hiv", a_blk, running_state, precision=PRECISION_LEVEL) + b_blk
        )
        return (running_state, final_result)

    last_state, outs = lax.scan(emit_block, start_state, (amat, bmat, out_zero, gmat))
    final_result = outs.transpose(0, 2, 1, 3).reshape(tokens, HV * DV).astype(jnp.bfloat16)
    return final_result[None]


def solution(mesh):
    return jax.shard_map(
        on_device,
        mesh=mesh,
        in_specs=(
            P("ea", "sa", None),
            P("ea", None, None),
            P("ea", "sa", None),
            P("ea", "sa", None),
            P("ea", "sa", None),
            P(),
            P("ea", None),
            P("ea", "sa", None),
            P("ea", "sa", None),
            P("ea", "sa", None),
            P("ea", "sa", None),
        ),
        out_specs=P("ea", "sa", None),
        check_vma=False,
    )
```

profile of v0, /device:TPU:15, one launch (start us, length us, event | category | flops | bytes accessed | tf_op | source)
XLA Modules:
  0.0 444.6 jit_solution(13216612535024970762)
XLA Ops:
  6.5 0.7 all-gather.6.cloned.1.call-update
  7.3 0.8 copy-done
  8.0 7.6 %convolution_convert_fusion = bf16[4,448,2048]{2,1,0:T(8,128)(2,1)S(1)} fusion(bf16[4,448,512]{2,1,0:T(8,128)(2,1)S(1)} %copy-done, bf16[4,512,2048]{2,1,0:T(8,128)(2,1)} %param.18), kind=kOutput, calls=%fused_computation.33 | convolution fusion | flops 3761766400 | bytes 17563648 | tf_op jit(solution)/shard_map/erf,efd->erd/dot_general | solution.py:62
  15.6 4.6 %copy.59 = bf16[4,8,56,2048]{3,2,0,1:T(8,128)(2,1)} copy(bf16[4,8,56,2048]{3,2,1,0:T(8,128)(2,1)S(1)} %bitcast.140) | data formatting | bytes 14680064 | tf_op jit(solution)/shard_map/reshape | solution.py:65
  20.2 5.8 %all-to-all-start = ((bf16[4,8,56,2048]{3,2,0,1:T(8,128)(2,1)}), bf16[4,8,56,2048]{3,2,0,1:T(8,128)(2,1)}, u32[]{:S(2)}, u32[]{:S(2)}) async-start(bf16[4,8,56,2048]{3,2,0,1:T(8,128)(2,1)} %copy.59), calls=%async_computation | async-start | bytes 14680064 | tf_op jit(solution)/shard_map/all_to_all | solution.py:85
  26.1 0.2 all-gather.8.cloned.1.call-start
  26.3 0.1 fusion.61
  26.7 0.1 convert_element_type.113
  26.9 0.1 mul.179
  27.1 0.1 copy.58
  27.7 0.2 multiply_reduce_fusion.2
  27.9 0.2 broadcast_multiply_fusion
  28.3 0.5 reduce_window_sum.11
  29.0 1.9 fusion.35
  30.9 158.0 %custom-call.4 = f32[2,16,1,64,64]{3,4,2,1,0:T(8,128)} custom-call(f32[2,16,1,64,64]{4,3,2,1,0:T(8,128)S(1)} %fusion.35), custom_call_target="InvertDiagBlocksLowerTriangular" | custom-call | tf_op jit(solution)/shard_map/jit(_solve_triangular)/vmap(vmap())/triangular_solve | solution.py:124
  188.8 0.2 slice_reduce_fusion
  189.1 89.9 %all-to-all-done = bf16[4,8,56,2048]{3,2,0,1:T(8,128)(2,1)} async-done(((bf16[4,8,56,2048]{3,2,0,1:T(8,128)(2,1)}), bf16[4,8,56,2048]{3,2,0,1:T(8,128)(2,1)}, u32[]{:S(2)}, u32[]{:S(2)}) %all-to-all-start) | async-done | bytes 7340064 | tf_op jit(solution)/shard_map/all_to_all | solution.py:85
  279.0 14.8 %gather_fusion = bf16[1280,2048]{1,0:T(8,128)(2,1)} fusion(bf16[1792,2048]{1,0:T(8,128)(2,1)} %bitcast.16, s32[2048]{0:T(1024)S(1)} %pad_clamp_fusion), kind=kCustom, calls=%fused_computation | custom fusion | bytes 10490880 | tf_op jit(solution)/shard_map/jit(_take)/gather | solution.py:82
  293.8 9.5 %gather.7 = bf16[128,10,2048]{2,1,0:T(8,128)(2,1)} reshape(bf16[1280,2048]{1,0:T(8,128)(2,1)} %gather_fusion) | data formatting | bytes 10485760 | tf_op jit(solution)/shard_map/jit(_take)/gather | solution.py:82
  303.4 9.2 %multiply_reduce_fusion = f32[128,2048]{1,0:T(8,128)S(1)} fusion(bf16[128,10,2048]{2,1,0:T(8,128)(2,1)} %gather.7, f32[128,10]{1,0:T(8,128)S(1)} %bitcast.147, pred[128,10]{1,0:T(8,128)(4,1)S(1)} %copy.58), kind=kLoop, calls=%fused_computation.32 | loop fusion | flops 10223616 | bytes 6297856 | tf_op jit(solution)/shard_map/reduce_sum | solution.py:83
  312.6 0.2 fusion.36
  312.9 4.7 %convolution_convert_fusion.1 = bf16[128,2048]{1,0:T(8,128)(2,1)S(1)} fusion(bf16[2048,2048]{1,0:T(8,128)(2,1)} %all-gather.6.cloned.1.call-done, bf16[128,2048]{1,0:T(8,128)(2,1)S(1)} %fusion.39, f32[2048]{0:T(1024)S(1)} %convert_element_type.117, f32[128]{0:T(128)S(1)} %add_rsqrt_fusion.2), kind=kOutput, calls=%fused_computation.34 | convolution fusion | flops 1075052544 | bytes 9445888 | tf_op jit(solution)/shard_map/dot_general | solution.py:94
  317.7 0.2 copy.71
  317.9 0.6 bitcast_multiply_fusion.1
  318.5 0.6 copy-done.11
  319.1 2.0 fusion.27
  321.1 5.2 %fusion.44 = f32[2,16,128,128]{3,2,1,0:T(8,128)} fusion(f32[2,16,64,256]{3,2,1,0:T(8,128)S(1)} %fusion.27, f32[2,64,16,128]{3,1,0,2:T(8,128)S(1)} %bitcast.135, f32[2,16,64]{2,1,0:T(8,128)S(1)} %get-tuple-element.240), kind=kOutput, calls=%fused_computation.65 | convolution fusion | flops 402915328 | bytes 4210688 | tf_op jit(solution)/shard_map/nhck,nhcv->nhkv/dot_general | solution.py:132
  326.3 4.0 multiply_subtract_fusion
  330.3 0.3 broadcast_in_dim.63
  330.6 10.7 %while.40 = (s32[]{:T(128)}, f32[16,128,128]{2,1,0:T(8,128)S(1)}, f32[16,128,128]{2,1,0:T(8,128)}, f32[2,16,128,128]{3,2,1,0:T(8,128)S(1)}, f32[2,16,128,128]{3,2,1,0:T(8,128)}, /*index=5*/s32[]{:T(128)}, s32[]{:T(128)}) while((s32[]{:T(128)}, f32[16,128,128]{2,1,0:T(8,128)S(1)}, f32[16,128,128]{2,1,0:T(8,128)}, ...), condition=%wide.region_7.8_spmd.clone, body=%wide.region_6.7_spmd.clone.sunk | while | flops 805830656 | bytes 19924088 | solution.py:144
  330.7 1.4 copy.139
  332.0 0.5 copy-done.2
  332.6 2.2 convolution_add_fusion.7
  334.8 1.2 fusion.99
  336.0 1.4 copy.139
  337.4 0.5 copy-done.2
  337.9 2.2 convolution_add_fusion.7
  340.2 1.2 fusion.99
  341.4 1.0 copy-done.4
  342.5 0.7 all-gather.10.cloned.1.call-update
  343.4 0.2 multiply_reduce_fusion.1
  343.6 0.2 multiply_multiply_fusion
  344.0 0.5 copy-done.6
  344.6 1.8 convolution_multiply_fusion
  346.4 2.2 fusion.45
  348.6 2.3 convolution_subtract_fusion
  350.9 27.2 %all-gather.8.cloned.1.call-done = f32[64,128,128]{2,1,0:T(8,128)} async-done(((f32[16,128,128]{2,1,0:T(8,128)}), f32[64,128,128]{2,1,0:T(8,128)}) %all-gather.8.cloned.1.call-update) | async-done | bytes 4194320 | tf_op jit(solution)/shard_map/all_gather | solution.py:18
  378.1 36.1 %all-gather.10.cloned.1.call-done = f32[64,128,128]{2,1,0:T(8,128)} async-done(((f32[16,128,128]{2,1,0:T(8,128)}), f32[64,128,128]{2,1,0:T(8,128)}) %all-gather.10.cloned.1.call-update) | async-done | bytes 4194320 | tf_op jit(solution)/shard_map/all_gather | solution.py:18
  414.2 11.7 %while.41 = (s32[]{:T(128)}, f32[16,128,128]{2,1,0:T(8,128)S(1)}, s32[]{:T(128)}, f32[4,16,128,128]{3,2,1,0:T(8,128)}, f32[4,16,128,128]{3,2,1,0:T(8,128)}, /*index=5*/s32[]{:T(128)}, s32[]{:T(128)}) while((s32[]{:T(128)}, f32[16,128,128]{2,1,0:T(8,128)S(1)}, s32[]{:T(128)}, f32[4,16,128,128]{3,2,1,0:T(8,128)}, ...), condition=%wide.region_9.10_spmd.clone, body=%wide.region_8.9_spmd.clone.sunk | while | flops 403701760 | bytes 7342687 | solution.py:30
  414.3 2.8 fusion.102
  417.2 2.8 fusion.102
  420.2 2.8 fusion.102
  423.1 2.8 fusion.102
  425.9 9.2 %while.39 = (s32[]{:T(128)}, f32[16,128,128]{2,1,0:T(8,128)S(1)}, bf16[2,16,64,128]{3,2,1,0:T(8,128)(2,1)}, f32[2,16,128,128]{3,2,1,0:T(8,128)S(1)}, f32[2,16,12...) while((s32[]{:T(128)}, f32[16,128,128]{2,1,0:T(8,128)S(1)}, ...), condition=%wide.region_12.13_spmd, body=%wide.region_11.12_spmd.sunk | while | flops 604372992 | bytes 25692328 | solution.py:158
  426.1 1.1 copy-done.9
  427.2 0.3 copy-done.10
  427.5 1.8 fusion.94
  429.3 1.2 convolution_add_fusion.6
  430.6 1.1 copy-done.9
  431.8 0.3 copy-done.10
  432.1 1.8 fusion.94
  433.9 1.2 convolution_add_fusion.6
  435.1 1.5 copy.66
  436.7 1.0 convert_element_type.124
  (89 shorter events, 2.6 us)
Async XLA Ops:
  6.5 1.5 copy-start
  6.5 306.3 %all-gather.6.cloned.1.call-start = ((), (), s32[]{:S(2)}) async-start(), calls=%async_computation.1 | async-start | bytes 9437184 | tf_op jit(solution)/shard_map/all_gather | solution.py:96
  20.2 6.0 %copy-start.15 = (s32[1,128,10]{1,0,2:T(1,128)S(1)}, s32[1,128,10]{1,0,2:T(1,128)}, u32[]{:S(2)}) copy-start(s32[1,128,10]{1,0,2:T(1,128)} %param.20) | copy-start | bytes 15364
  20.2 7.0 %copy-start.18 = (f32[1,128,10]{1,0,2:T(1,128)S(1)}, f32[1,128,10]{1,0,2:T(1,128)}, u32[]{:S(2)}) copy-start(f32[1,128,10]{1,0,2:T(1,128)} %param.21) | copy-start | bytes 15364
  20.2 7.1 %copy-start.19 = (bf16[2048]{0:T(1024)(128)(2,1)S(1)}, bf16[2048]{0:T(1024)(128)(2,1)}, u32[]{:S(2)}) copy-start(bf16[2048]{0:T(1024)(128)(2,1)} %param.22) | copy-start | bytes 12292
  20.2 7.1 %copy-start.16 = (f32[1,128,16]{1,2,0:T(8,128)S(1)}, f32[1,128,16]{1,2,0:T(8,128)}, u32[]{:S(2)}) copy-start(f32[1,128,16]{1,2,0:T(8,128)} %param.26) | copy-start | bytes 24580
  20.2 7.2 %copy-start.17 = (f32[1,128,16]{1,2,0:T(8,128)S(1)}, f32[1,128,16]{1,2,0:T(8,128)}, u32[]{:S(2)}) copy-start(f32[1,128,16]{1,2,0:T(8,128)} %param.27) | copy-start | bytes 24580
  20.2 7.3 %copy-start.13 = (bf16[1,128,1024]{2,1,0:T(8,128)(2,1)S(1)}, bf16[1,128,1024]{2,1,0:T(8,128)(2,1)}, u32[]{:S(2)}) copy-start(bf16[1,128,1024]{2,1,0:T(8,128)(2,1)} %param.25) | copy-start | bytes 786436
  20.2 258.7 %all-to-all-start = ((bf16[4,8,56,2048]{3,2,0,1:T(8,128)(2,1)}), bf16[4,8,56,2048]{3,2,0,1:T(8,128)(2,1)}, u32[]{:S(2)}, u32[]{:S(2)}) async-start(bf16[4,8,56,2048]{3,2,0,1:T(8,128)(2,1)} %copy.59), calls=%async_computation | async-start | bytes 14680064 | tf_op jit(solution)/shard_map/all_to_all | solution.py:85
  26.1 352.1 %all-gather.8.cloned.1.call-start = ((), (), s32[]{:S(2)}) async-start(), calls=%async_computation.2 | async-start | bytes 5242880 | tf_op jit(solution)/shard_map/all_gather | solution.py:18
  28.9 297.3 %copy-start.5 = (f32[128,8,2,128]{3,0,2,1:T(8,128)}, f32[128,8,2,128]{3,0,2,1:T(8,128)S(1)}, u32[]{:S(2)}) copy-start(f32[128,8,2,128]{3,0,2,1:T(8,128)S(1)} %broadcast_in_dim.64) | copy-start | bytes 3145732
  303.4 9.2 %copy-start.12 = (bf16[1,128,2048]{2,1,0:T(8,128)(2,1)S(1)}, bf16[1,128,2048]{2,1,0:T(8,128)(2,1)}, u32[]{:S(2)}) copy-start(bf16[1,128,2048]{2,1,0:T(8,128)(2,1)} %param.19) | copy-start | bytes 1572868
  317.9 1.2 copy-start.11
  321.1 5.2 %copy-start.7 = (f32[2,16,64,256]{3,2,1,0:T(8,128)}, f32[2,16,64,256]{3,2,1,0:T(8,128)S(1)}, u32[]{:S(2)}) copy-start(f32[2,16,64,256]{3,2,1,0:T(8,128)S(1)} %fusion.27) | copy-start | bytes 6291460
  330.6 1.9 copy-start.2
  336.0 1.9 copy-start.2
  341.3 1.1 copy-start.4
  341.4 1.8 copy-start.14
  342.4 71.8 %all-gather.10.cloned.1.call-start = ((), (), s32[]{:S(2)}) async-start(), calls=%async_computation.3 | async-start | bytes 5242880 | tf_op jit(solution)/shard_map/all_gather | solution.py:18
  343.3 1.2 copy-start.6
  343.9 2.5 copy-start.8
  426.0 1.2 copy-start.9
  426.0 1.5 copy-start.10
  426.0 3.3 copy-start.3
  430.5 1.2 copy-start.9
  430.6 1.5 copy-start.10
  430.6 3.3 copy-start.3
  435.1 2.6 copy-start.1
Sparse Core Ops, SparseCore 0:
  9.5 244.3 all-gather.5
  342.5 35.5 all-gather.7
  379.7 34.4 all-gather.9
where the time goes:
time: 450 us; the launch traced here: 445 us
  other arithmetic  170 us (38%)
  waiting for transfers between devices  155 us (34%)
  matrix products  55.8 us (12%)
  local copies, waits for them, and re-layouts  44 us (10%)
  between operations  14 us (3%)
  starting transfers between devices  6.04 us (1%)
    another operation x4, other arithmetic, on_device(): jax.scipy.linalg.solve_triangular(system, rhs, lower=True, unit_diagonal=...  158 us
    all_to_all x1, waiting for transfers between devices, on_device(): lax.all_to_all(produced, 'ea', split_axis=1, concat_axis=0, tiled=True)  89.9 us
    all_gather x2, waiting for transfers between devices, carried_in(): everything = jax.tree.map(lambda part: lax.all_gather(part, axis), shard)  63.3 us
    gather x2, local copies, waits for them, and re-layouts, combine(): picked = jnp.take(flat, rows, axis=0).reshape(tokens, top, flat.shape[1])  24.4 us
    dot_general x6, matrix products, compose(): jnp.einsum('hij,hjk->hik', later[0], earlier[1], precision=PRECISION_LEVEL)  15.6 us
    reduce_sum x1, other arithmetic, combine(): return jnp.sum(weights[:, :, None] * picked.astype(jnp.float32), axis=1)  9.15 us
  transfers between devices with their start and end apart: 4, of which 3 were waited for; matrix products, arithmetic and copies ran while one was open for 49% of the time, Pallas kernels for 0%

commit v1 on v0

v1 whole, which is shorter than its diff:
```python
import functools

import jax
import jax.numpy as jnp
from jax import lax
from jax.experimental import pallas as pl
from jax.experimental.pallas import tpu as pltpu
from jax.sharding import PartitionSpec as P

HV = 16
HK = 8
DK = 128
DV = 128
F32 = jnp.float32
BF16 = jnp.bfloat16
VMEM_BYTES = 60 * 1024 * 1024


def dot1(a, b):
    return jnp.dot(a.astype(BF16), b.astype(BF16), preferred_element_type=F32)


def split(a):
    high = a.astype(BF16)
    return high, (a - high.astype(F32)).astype(BF16)


def dot3(a, b):
    ah, al = split(a)
    bh, bl = split(b)
    d = functools.partial(jnp.dot, preferred_element_type=F32)
    return d(ah, bh) + (d(ah, bl) + d(al, bh))


def iotas(rows, columns):
    return (
        lax.broadcasted_iota(jnp.int32, (rows, columns), 0),
        lax.broadcasted_iota(jnp.int32, (rows, columns), 1),
    )


def expert_kernel(exp_dev, n_seq, pad, hidden_ref, down_ref, named_ref, out_ref, mix_ref, made_ref):
    tokens, top = out_ref.shape[1], named_ref.shape[2] // 2
    width = out_ref.shape[2]

    @pl.when(pl.program_id(0) == 0)
    def _():
        first = lax.axis_index("ea") * exp_dev
        row, col = iotas(tokens, tokens)
        before = (row > col).astype(BF16)
        place = lax.broadcasted_iota(jnp.int32, (tokens, pad), 1).astype(F32)

        def mix(s, carry):
            named = named_ref[s]
            ids, weights = named[:, :top], named[:, top:]
            parts = []
            for e in range(exp_dev):
                hit = ids == (first + e).astype(F32)
                count = jnp.sum(hit.astype(F32), axis=1, keepdims=True)
                weight = jnp.sum(jnp.where(hit, weights, 0.0), axis=1, keepdims=True)
                slot = jnp.dot(
                    before,
                    jnp.broadcast_to(count, (tokens, pad)).astype(BF16),
                    preferred_element_type=F32,
                )
                parts.append(jnp.where((slot == place) & (count > 0.0), weight, 0.0))
            mix_ref[s] = jnp.concatenate(parts, axis=1).astype(BF16)
            return carry

        lax.fori_loop(0, n_seq, mix, 0)

    for e in range(exp_dev):
        made = jnp.dot(
            hidden_ref[e], down_ref[e], preferred_element_type=F32
        ).astype(BF16)
        made_ref[:, pl.ds(e * pad, pad), :] = made.reshape(n_seq, pad, width)

    def emit(s, carry):
        out_ref[s] = jnp.dot(mix_ref[s], made_ref[s], preferred_element_type=F32).astype(
            out_ref.dtype
        )
        return carry

    lax.fori_loop(0, n_seq, emit, 0)


def expert_partials(hidden, down, named, n_seq, tokens):
    exp_dev, rows, ff_units = hidden.shape
    width = down.shape[2]
    pad = rows // n_seq
    tile = min(width, 512)
    return pl.pallas_call(
        functools.partial(expert_kernel, exp_dev, n_seq, pad),
        grid=(width // tile,),
        out_shape=jax.ShapeDtypeStruct((n_seq, tokens, width), BF16),
        in_specs=[
            pl.BlockSpec((exp_dev, rows, ff_units), lambda n: (0, 0, 0)),
            pl.BlockSpec((exp_dev, ff_units, tile), lambda n: (0, 0, n)),
            pl.BlockSpec(named.shape, lambda n: (0, 0, 0)),
        ],
        out_specs=pl.BlockSpec((n_seq, tokens, tile), lambda n: (0, 0, n)),
        scratch_shapes=[
            pltpu.VMEM((n_seq, tokens, exp_dev * pad), BF16),
            pltpu.VMEM((n_seq, exp_dev * pad, tile), BF16),
        ],
        compiler_params=pltpu.CompilerParams(vmem_limit_bytes=VMEM_BYTES),
        cost_estimate=pl.CostEstimate(
            flops=2 * exp_dev * rows * width * (ff_units + tokens),
            bytes_accessed=2 * (hidden.size + down.size + n_seq * tokens * width),
            transcendentals=0,
        ),
        name="experts",
    )(hidden, down, named)


def maps_kernel(q_ref, k_ref, decay_ref, decay_t_ref, rate_ref, rate_t_ref, mn_ref, ga_ref, sum_ref, sum_t_ref):
    kh = pl.program_id(0)
    tokens = q_ref.shape[0]
    row, col = iotas(tokens, tokens)
    inclusive, strict = row >= col, row > col

    @pl.when(kh == 0)
    def _():
        exact = functools.partial(
            jnp.dot, precision=lax.Precision.HIGHEST, preferred_element_type=F32
        )
        sum_ref[...] = exact(inclusive.astype(F32), decay_ref[...])
        sum_t_ref[...] = exact(decay_t_ref[...], (row <= col).astype(F32))

    def unit(x):
        x = x.astype(F32)
        return x * lax.rsqrt(jnp.sum(x * x, axis=-1, keepdims=True) + 1e-06)

    kn = unit(k_ref[...])
    qn = unit(q_ref[...]) * DK ** (-0.5)
    kn_t = kn.T
    pairs = dot3(jnp.concatenate([kn, qn], axis=0), kn_t)
    kk, qk = pairs[:tokens], pairs[tokens:]
    per = HV // HK
    sums, rates = sum_ref[...], rate_ref[...]
    lane = lax.broadcasted_iota(jnp.int32, sums.shape, 1)
    levels = []
    size = 1
    while size < tokens:
        levels.append(size)
        size *= 2
    state = []
    for u in range(per):
        h = kh * per + u
        s_col = jnp.sum(jnp.where(lane == h, sums, 0.0), axis=1, keepdims=True)
        b_col = jnp.sum(jnp.where(lane == h, rates, 0.0), axis=1, keepdims=True)
        s_row, b_row = sum_t_ref[pl.ds(h, 1), :], rate_t_ref[pl.ds(h, 1), :]
        ratio = jnp.where(inclusive, jnp.exp(jnp.where(inclusive, s_col - s_row, 0.0)), 0.0)
        lower = jnp.where(strict, b_col * ratio * kk, 0.0)
        state.append([s_col, s_row, b_row, ratio, lower, (row == col).astype(F32)])
    for size in levels:
        joins = (row // (2 * size) == col // (2 * size)) & (row // size != col // size)
        for st in state:
            link = jnp.where(joins, st[4], 0.0)
            if size == 1:
                st[5] = st[5] - link
            else:
                st[5] = st[5] - dot3(st[5], dot3(link, st[5]))
    for u, (s_col, s_row, b_row, ratio, lower, inverse) in enumerate(state):
        last = s_row[:, tokens - 1 :]
        growth = jnp.exp(s_col)
        both = jnp.concatenate([qk * ratio, kn_t * jnp.exp(last - s_row)], axis=0)
        mn = dot3(both, inverse) * b_row
        base = jnp.concatenate(
            [growth * qn, jnp.where(row == col, jnp.exp(last), 0.0)], axis=0
        )
        ga = base - dot3(mn, growth * kn)
        mn_ref[u] = mn.astype(BF16)
        ga_ref[u] = ga.astype(BF16)


def head_maps(queries, keys, decay, rate):
    tokens = queries.shape[0]
    per = HV // HK
    whole = lambda shape: pl.BlockSpec(shape, lambda h: (0, 0))
    out = jax.ShapeDtypeStruct((HV, tokens + DK, DK), BF16)
    return pl.pallas_call(
        maps_kernel,
        grid=(HK,),
        out_shape=(out, out),
        in_specs=[
            pl.BlockSpec((tokens, DK), lambda h: (0, h)),
            pl.BlockSpec((tokens, DK), lambda h: (0, h)),
            whole((tokens, HV)),
            whole((HV, tokens)),
            whole((tokens, HV)),
            whole((HV, tokens)),
        ],
        out_specs=[pl.BlockSpec((per, tokens + DK, DK), lambda h: (h, 0, 0))] * 2,
        scratch_shapes=[pltpu.VMEM((tokens, HV), F32), pltpu.VMEM((HV, tokens), F32)],
        compiler_params=pltpu.CompilerParams(vmem_limit_bytes=VMEM_BYTES),
        cost_estimate=pl.CostEstimate(
            flops=HV * 64 * 2 * tokens * tokens * DK,
            bytes_accessed=6 * tokens * HV * DK * 2,
            transcendentals=HV * tokens * tokens,
        ),
        name="maps",
    )(queries, keys, decay, decay.T, rate, rate.T)


def value_kernel(res_ref, moe_ref, gain_ref, weight_ref, mn_ref, out_ref, state_ref, normed_ref):
    tokens = res_ref.shape[0]

    @pl.when(pl.program_id(0) == 0)
    def _():
        stream = (res_ref[...].astype(F32) + moe_ref[...].astype(F32)).astype(BF16).astype(F32)
        scale = lax.rsqrt(jnp.mean(stream * stream, axis=-1, keepdims=True) + 1e-06)
        normed_ref[...] = (stream * scale * gain_ref[...].astype(F32)).astype(BF16)

    values = jnp.dot(normed_ref[...], weight_ref[...], preferred_element_type=F32).astype(BF16)
    for u in range(mn_ref.shape[0]):
        both = jnp.dot(
            mn_ref[u], values[:, u * DV : (u + 1) * DV], preferred_element_type=F32
        )
        out_ref[:, u * DV : (u + 1) * DV] = both[:tokens]
        state_ref[u] = both[tokens:].astype(BF16)


def value_heads(residual, moe, gain, weight, mn):
    tokens, width = residual.shape
    per = 4
    tile = per * DV
    whole = lambda shape: pl.BlockSpec(shape, lambda n: (0, 0))
    return pl.pallas_call(
        value_kernel,
        grid=(HV // per,),
        out_shape=(
            jax.ShapeDtypeStruct((tokens, HV * DV), F32),
            jax.ShapeDtypeStruct((HV, DK, DV), BF16),
        ),
        in_specs=[
            whole((tokens, width)),
            whole((tokens, width)),
            whole((1, width)),
            pl.BlockSpec((width, tile), lambda n: (0, n)),
            pl.BlockSpec((per, tokens + DK, DK), lambda n: (n, 0, 0)),
        ],
        out_specs=[
            pl.BlockSpec((tokens, tile), lambda n: (0, n)),
            pl.BlockSpec((per, DK, DV), lambda n: (n, 0, 0)),
        ],
        scratch_shapes=[pltpu.VMEM((tokens, width), BF16)],
        compiler_params=pltpu.CompilerParams(vmem_limit_bytes=VMEM_BYTES),
        cost_estimate=pl.CostEstimate(
            flops=2 * tokens * width * HV * DV,
            bytes_accessed=2 * (weight.size + 6 * tokens * width),
            transcendentals=0,
        ),
        name="values",
    )(residual, moe, gain.reshape(1, width), weight, mn)


def close_kernel(maps_ref, states_ref, ga_ref, zero_ref, out_ref):
    n_sa, per = maps_ref.shape[:2]
    tokens = zero_ref.shape[0]
    here = lax.axis_index("sa")
    for u in range(per):
        state = jnp.zeros((DK, DV), F32)
        for i in range(n_sa - 1):
            new = states_ref[i, u].astype(F32)
            if i > 0:
                new = new + dot1(maps_ref[i, u], state)
            state = jnp.where(i < here, new, state)
        cols = slice(u * DV, (u + 1) * DV)
        out_ref[:, cols] = (zero_ref[:, cols] + dot1(ga_ref[u, :tokens], state)).astype(BF16)


def close_heads(maps, states, ga, zero):
    n_sa = maps.shape[0]
    tokens = zero.shape[0]
    per = 4
    gathered = pl.BlockSpec((n_sa, per, DK, DK), lambda n: (0, n, 0, 0))
    return pl.pallas_call(
        close_kernel,
        grid=(HV // per,),
        out_shape=jax.ShapeDtypeStruct((tokens, HV * DV), BF16),
        in_specs=[
            gathered,
            gathered,
            pl.BlockSpec((per, tokens + DK, DK), lambda n: (n, 0, 0)),
            pl.BlockSpec((tokens, per * DV), lambda n: (0, n)),
        ],
        out_specs=pl.BlockSpec((tokens, per * DV), lambda n: (0, n)),
        compiler_params=pltpu.CompilerParams(vmem_limit_bytes=VMEM_BYTES),
        cost_estimate=pl.CostEstimate(
            flops=HV * n_sa * 2 * DK * DK * DV,
            bytes_accessed=2 * (2 * maps.size + ga.size + 3 * zero.size),
            transcendentals=0,
        ),
        name="close",
    )(maps, states, ga, zero)


def on_device(
    expert_hidden,
    down_weight,
    residual,
    expert_ids,
    combine_weight,
    norm_gain,
    value_weight,
    queries,
    keys,
    log_decay,
    write_rate,
):
    n_ea = lax.axis_size("ea")
    exp_dev, rows, ff_units = expert_hidden.shape
    cap = rows // n_ea
    tokens = residual.shape[1]
    pad = -(-cap // 16) * 16
    hidden = jnp.pad(
        expert_hidden.reshape(exp_dev, n_ea, cap, ff_units), ((0, 0), (0, 0), (0, pad - cap), (0, 0))
    ).reshape(exp_dev, n_ea * pad, ff_units)
    named = jnp.concatenate([expert_ids[0].astype(F32), combine_weight[0]], axis=-1)
    named = lax.all_gather(named, "ea")
    weight = lax.all_gather(value_weight, "ea", axis=0, tiled=True)
    partial = expert_partials(hidden, down_weight, named, n_ea, tokens)
    moe = lax.psum_scatter(partial, "ea", scatter_dimension=0, tiled=True)[0]
    mn, ga = head_maps(queries[0], keys[0], log_decay[0], write_rate[0])
    maps = lax.all_gather(ga[:, tokens:], "sa")
    zero, state = value_heads(residual[0], moe, norm_gain, weight, mn)
    states = lax.all_gather(state, "sa")
    return close_heads(maps, states, ga, zero)[None]


def solution(mesh):
    return jax.shard_map(
        on_device,
        mesh=mesh,
        in_specs=(
            P("ea", "sa", None),
            P("ea", None, None),
            P("ea", "sa", None),
            P("ea", "sa", None),
            P("ea", "sa", None),
            P(),
            P("ea", None),
            P("ea", "sa", None),
            P("ea", "sa", None),
            P("ea", "sa", None),
            P("ea", "sa", None),
        ),
        out_specs=P("ea", "sa", None),
        check_vma=False,
    )
```

time: 450 us -> 337 us (0.75)
  other arithmetic: 170 us -> 0.7 us
  waiting for transfers between devices: 155 us -> 233 us
  Pallas kernels: 0 us -> 57.3 us
  matrix products: 55.8 us -> 0 us
  local copies, waits for them, and re-layouts: 44 us -> 8.78 us
  blocking collectives: 0 us -> 21.8 us
  starting transfers between devices: 6.04 us -> 0.12 us
    another operation x5 -> x0, other arithmetic: 159 us -> none  [the longest x4 158 us: on_device(): jax.scipy.linalg.solve_triangular(system, rhs, lower=True, unit_diagonal=...]
    all_gather x3, waiting for transfers between devices: 63.3 us -> 165 us  [the longest x1 123 us: on_device(): weight = lax.all_gather(value_weight, 'ea', axis=0, tiled=True)]
    all_to_all x1 -> x0, waiting for transfers between devices: 89.9 us -> none  [on_device(): lax.all_to_all(produced, 'ea', split_axis=1, concat_axis=0, tiled=True)]
    reduce_scatter x0 -> x1, waiting for transfers between devices: none -> 66.6 us  [on_device(): moe = lax.psum_scatter(partial, 'ea', scatter_dimension=0, tiled=True)[0]]
    pallas_call x0 -> x4, Pallas kernels: none -> 57.3 us  [the longest x1 26.6 us: head_maps(): pl.pallas_call(maps_kernel, grid=(HK,), out_shape=(out, out), in_specs=[p...]
    dot_general x21 -> x0, matrix products: 53.7 us -> none  [the longest x6 15.6 us: compose(): jnp.einsum('hij,hjk->hik', later[0], earlier[1], precision=PRECISION_LEVEL)]
    gather x2 -> x0, local copies, waits for them, and re-layouts: 24.4 us -> none  [combine(): picked = jnp.take(flat, rows, axis=0).reshape(tokens, top, flat.shape[1])]
    all_gather x0 -> x1, blocking collectives: none -> 21.8 us  [on_device(): named = lax.all_gather(named, 'ea')]
  transfers between devices with their start and end apart: 4 -> 4, of which waited for: 3 -> 4; matrix products, arithmetic and copies ran while one was open for 49% -> 1% of each run, Pallas kernels for 0% -> 10%
where the time goes in v1:
time: 337 us; the launch traced here: 335 us
  waiting for transfers between devices  233 us (69%)
  Pallas kernels  57.3 us (17%)
  blocking collectives  21.8 us (6%)
  between operations  13.1 us (4%)
  local copies, waits for them, and re-layouts  8.78 us (3%)
    all_gather x1, waiting for transfers between devices, on_device(): weight = lax.all_gather(value_weight, 'ea', axis=0, tiled=True)  123 us
    reduce_scatter x1, waiting for transfers between devices, on_device(): moe = lax.psum_scatter(partial, 'ea', scatter_dimension=0, tiled=True)[0]  66.6 us
    pallas_call x1, Pallas kernels, head_maps(): pl.pallas_call(maps_kernel, grid=(HK,), out_shape=(out, out), in_specs=[p...  26.6 us
    all_gather x1, waiting for transfers between devices, on_device(): states = lax.all_gather(state, 'sa')  24 us
    all_gather x1, blocking collectives, on_device(): named = lax.all_gather(named, 'ea')  21.8 us
    all_gather x1, waiting for transfers between devices, on_device(): maps = lax.all_gather(ga[:, tokens:], 'sa')  18.3 us
    pallas_call x1, Pallas kernels, expert_partials(): pl.pallas_call(functools.partial(expert_kernel, exp_dev, n_seq, pad), gri...  17.5 us
    pallas_call x1, Pallas kernels, value_heads(): pl.pallas_call(value_kernel, grid=(HV // per,), out_shape=(jax.ShapeDtype...  7.01 us
  transfers between devices with their start and end apart: 4, of which 4 were waited for; matrix products, arithmetic and copies ran while one was open for 1% of the time, Pallas kernels for 10%

profile of v1, /device:TPU:15, one launch (start us, length us, event | category | flops | bytes accessed | tf_op | source)
XLA Modules:
  0.0 334.5 jit_solution(1279872870632441098)
XLA Ops:
  6.5 0.0 reduce-scatter.2.cloned.1.call-start
  6.5 0.7 copy.25
  7.2 0.7 fusion
  7.9 21.8 %all-gather.1 = f32[1024,20]{0,1:T(8,128)S(1)} all-gather(f32[128,20]{0,1:T(8,128)S(1)} %pad_maximum_fusion), channel_id=3, replica_groups=mesh['ea'=8,'sa'=4] {'ea'}, dimensions={0}, use_global_device_ids=true | all-gather | bytes 92160 | tf_op jit(solution)/shard_map/all_gather | solution.py:321
  29.7 1.0 copy.19
  30.8 3.1 pad.4
  33.9 17.5 %experts.1 = bf16[8,128,2048]{2,1,0:T(8,128)(2,1)} custom-call(bf16[4,512,512]{2,1,0:T(8,128)(2,1)} %bitcast.23, bf16[4,512,2048]{2,1,0:T(8,128)(2,1)} %down_ref.1, f32[8,128,20]{2,1,0:T(8,128)} %bitcast.27), custom_call_target="tpu_custom_call" | custom-call | flops 5368709120 | bytes 14680064 | tf_op jit(solution)/shard_map/experts/pallas_call | solution.py:92
  51.4 0.0 copy-start
  51.4 0.0 copy-start.1
  51.4 0.0 reduce-scatter.2.cloned.1.call-update
  51.4 0.0 all-gather.7.cloned.1.call-start
  51.4 0.7 all-gather.7.cloned.1.call-update
  52.1 0.0 all-gather.9.cloned.1.call-start
  52.2 0.0 copy-done
  52.2 0.7 copy.16.decay_ref
  52.9 0.0 copy-done.1
  52.9 0.7 copy.17.rate_ref
  53.7 0.0 copy-start.2
  53.7 26.6 %maps.1 = (bf16[16,256,128]{2,1,0:T(8,128)(2,1)}, bf16[16,256,128]{2,1,0:T(8,128)(2,1)}) custom-call(bf16[128,1024]{1,0:T(8,128)(2,1)} %bitcast.33, bf16[128,1024]{1,0:T(8,128)(2,1)} %bitcast.34, f32[128,16]{1,0:T(8,128)} %copy.16.decay_ref, f32[16,128]{1,0:T(8,128)} %bitcast.29, f32[128,16]{1,0:T(8,128)} %copy.17.rate_ref, f32[16,128]{1,0:T(8,128)} %bitcast.31), custom_call_target="tpu_custom_call" | custom-call | flops 4294967296 | bytes 3145728 | tf_op jit(solution)/shard_map/maps/pallas_call | solution.py:182
  80.3 1.9 slice.3
  82.2 0.0 all-gather.9.cloned.1.call-update
  82.2 0.0 all-gather.11.cloned.1.call-start
  82.3 0.0 copy-done.2
  82.3 0.6 reshape.12.gain_ref
  82.9 66.6 %reduce-scatter.2.cloned.1.call-done = bf16[1,128,2048]{2,1,0:T(8,128)(2,1)} async-done(((bf16[8,128,2048]{2,1,0:T(8,128)(2,1)}), bf16[1,128,2048]{2,1,0:T(8,128)(2,1)}) %reduce-scatter.2.cloned.1.call-update) | async-done | bytes 524304 | tf_op jit(solution)/shard_map/reduce_scatter | solution.py:324
  149.5 123.0 %all-gather.7.cloned.1.call-done.weight_ref = bf16[2048,2048]{1,0:T(8,128)(2,1)} async-done(((bf16[256,2048]{1,0:T(8,128)(2,1)}), bf16[2048,2048]{1,0:T(8,128)(2,1)}) %all-gather.7.cloned.1.call-update) | async-done | bytes 8388624 | tf_op jit(solution)/shard_map/all_gather | solution.py:322
  272.4 7.0 %values.1 = (f32[128,2048]{1,0:T(8,128)}, bf16[16,128,128]{2,1,0:T(8,128)(2,1)}) custom-call(bf16[128,2048]{1,0:T(8,128)(2,1)} %bitcast.25, bf16[128,2048]{1,0:T(8,128)(2,1)} %bitcast.26, bf16[1,2048]{1,0:T(2,128)(2,1)} %reshape.12.gain_ref, bf16[2048,2048]{1,0:T(8,128)(2,1)} %all-gather.7.cloned.1.call-done.weight_ref, ...), custom_call_target="tpu_custom_call" | custom-call | flops 1073741824 | bytes 11534336 | tf_op jit(solution)/shard_map/values/pallas_call | solution.py:229
  279.5 0.0 all-gather.11.cloned.1.call-update
  279.5 18.3 %all-gather.9.cloned.1.call-done = bf16[64,128,128]{2,1,0:T(8,128)(2,1)} async-done(((bf16[16,128,128]{2,1,0:T(8,128)(2,1)}), bf16[64,128,128]{2,1,0:T(8,128)(2,1)}) %all-gather.9.cloned.1.call-update) | async-done | bytes 2097168 | tf_op jit(solution)/shard_map/all_gather | solution.py:326
  297.8 24.0 %all-gather.11.cloned.1.call-done = bf16[64,128,128]{2,1,0:T(8,128)(2,1)} async-done(((bf16[16,128,128]{2,1,0:T(8,128)(2,1)}), bf16[64,128,128]{2,1,0:T(8,128)(2,1)}) %all-gather.11.cloned.1.call-update) | async-done | bytes 2097168 | tf_op jit(solution)/shard_map/all_gather | solution.py:328
  321.8 6.2 %close.1 = bf16[128,2048]{1,0:T(8,128)(2,1)} custom-call(bf16[4,16,128,128]{3,2,1,0:T(8,128)(2,1)} %bitcast.21, bf16[4,16,128,128]{3,2,1,0:T(8,128)(2,1)} %bitcast.22, bf16[16,256,128]{2,1,0:T(8,128)(2,1)} %get-tuple-element.9.ga_ref, f32[128,2048]{1,0:T(8,128)} %get-tuple-element.12.zero_ref), custom_call_target="tpu_custom_call" | custom-call | flops 268435456 | bytes 6815744 | tf_op jit(solution)/shard_map/close/pallas_call | solution.py:278
  (1 shorter events, 0.0 us)
Async XLA Ops:
  6.5 142.9 %reduce-scatter.2.cloned.1.call-start = ((), (), s32[]{:S(2)}) async-start(), calls=%async_computation.1 | async-start | bytes 4718592 | tf_op jit(solution)/shard_map/reduce_scatter | solution.py:324
  51.4 0.8 copy-start
  51.4 1.6 copy-start.1
  51.4 221.1 %all-gather.7.cloned.1.call-start = ((), (), s32[]{:S(2)}) async-start(), calls=%async_computation.2 | async-start | bytes 9437184 | tf_op jit(solution)/shard_map/all_gather | solution.py:322
  52.1 245.6 %all-gather.9.cloned.1.call-start = ((), (), s32[]{:S(2)}) async-start(), calls=%async_computation.3 | async-start | bytes 2621440 | tf_op jit(solution)/shard_map/all_gather | solution.py:326
  53.7 28.6 %copy-start.2 = (bf16[2048]{0:T(1024)(128)(2,1)S(1)}, bf16[2048]{0:T(1024)(128)(2,1)}, u32[]{:S(2)}) copy-start(bf16[2048]{0:T(1024)(128)(2,1)} %param.16) | copy-start | bytes 12292
  82.2 239.6 %all-gather.11.cloned.1.call-start = ((), (), s32[]{:S(2)}) async-start(), calls=%async_computation.4 | async-start | bytes 2621440 | tf_op jit(solution)/shard_map/all_gather | solution.py:328
Sparse Core Ops, SparseCore 0:
  51.5 97.9 reduce-scatter.1
  151.6 120.8 all-gather.6
  274.0 23.6 all-gather.8
  299.2 22.5 all-gather.10

commit v2 on v1

--- a/solution.py
+++ b/solution.py
@@ -14,6 +14,7 @@
 F32 = jnp.float32
 BF16 = jnp.bfloat16
 VMEM_BYTES = 60 * 1024 * 1024
+MESH = pl.DeviceIdType.MESH
 
 
 def dot1(a, b):
@@ -113,26 +114,27 @@
     )(hidden, down, named)
 
 
-def maps_kernel(q_ref, k_ref, decay_ref, decay_t_ref, rate_ref, rate_t_ref, mn_ref, ga_ref, sum_ref, sum_t_ref):
-    kh = pl.program_id(0)
-    tokens = q_ref.shape[0]
+def sum_decays(decay_ref, decay_t_ref, sum_ref, sum_t_ref):
+    tokens = decay_ref.shape[0]
+    row, col = iotas(tokens, tokens)
+    exact = functools.partial(
+        jnp.dot, precision=lax.Precision.HIGHEST, preferred_element_type=F32
+    )
+    sum_ref[...] = exact((row >= col).astype(F32), decay_ref[...])
+    sum_t_ref[...] = exact(decay_t_ref[...], (row <= col).astype(F32))
+
+
+def unit(x):
+    x = x.astype(F32)
+    return x * lax.rsqrt(jnp.sum(x * x, axis=-1, keepdims=True) + 1e-06)
+
+
+def key_head_maps(kh, q, k, rate_ref, rate_t_ref, sum_ref, sum_t_ref):
+    tokens = q.shape[0]
     row, col = iotas(tokens, tokens)
     inclusive, strict = row >= col, row > col
-
-    @pl.when(kh == 0)
-    def _():
-        exact = functools.partial(
-            jnp.dot, precision=lax.Precision.HIGHEST, preferred_element_type=F32
-        )
-        sum_ref[...] = exact(inclusive.astype(F32), decay_ref[...])
-        sum_t_ref[...] = exact(decay_t_ref[...], (row <= col).astype(F32))
-
-    def unit(x):
-        x = x.astype(F32)
-        return x * lax.rsqrt(jnp.sum(x * x, axis=-1, keepdims=True) + 1e-06)
-
-    kn = unit(k_ref[...])
-    qn = unit(q_ref[...]) * DK ** (-0.5)
+    kn = unit(k)
+    qn = unit(q) * DK ** (-0.5)
     kn_t = kn.T
     pairs = dot3(jnp.concatenate([kn, qn], axis=0), kn_t)
     kk, qk = pairs[:tokens], pairs[tokens:]
@@ -161,6 +163,7 @@
                 st[5] = st[5] - link
             else:
                 st[5] = st[5] - dot3(st[5], dot3(link, st[5]))
+    outs = []
     for u, (s_col, s_row, b_row, ratio, lower, inverse) in enumerate(state):
         last = s_row[:, tokens - 1 :]
         growth = jnp.exp(s_col)
@@ -170,8 +173,21 @@
             [growth * qn, jnp.where(row == col, jnp.exp(last), 0.0)], axis=0
         )
         ga = base - dot3(mn, growth * kn)
-        mn_ref[u] = mn.astype(BF16)
-        ga_ref[u] = ga.astype(BF16)
+        outs.append((mn.astype(BF16), ga.astype(BF16)))
+    return outs
+
+
+def maps_kernel(q_ref, k_ref, decay_ref, decay_t_ref, rate_ref, rate_t_ref, mn_ref, ga_ref, sum_ref, sum_t_ref):
+    kh = pl.program_id(0)
+
+    @pl.when(kh == 0)
+    def _():
+        sum_decays(decay_ref, decay_t_ref, sum_ref, sum_t_ref)
+
+    outs = key_head_maps(kh, q_ref[...], k_ref[...], rate_ref, rate_t_ref, sum_ref, sum_t_ref)
+    for u, (mn, ga) in enumerate(outs):
+        mn_ref[u] = mn
+        ga_ref[u] = ga
 
 
 def head_maps(queries, keys, decay, rate):
@@ -294,6 +310,297 @@
         ),
         name="close",
     )(maps, states, ga, zero)
+
+
+def gather_kernel(
+    cap, pad,
+    named_ref, hidden_hbm, down_hbm, res_ref, gain_ref, weight_ref, q_ref, k_ref,
+    decay_ref, decay_t_ref, rate_ref, rate_t_ref,
+    normed_ref, full_ref, mn_ref, ga_ref,
+    table_ref, hidden_ref, down_ref, made_ref, mix_ref, send_ref, got_ref, sum_ref, sum_t_ref,
+    load_sem, own_sem, sem_t, sem_w, sem_f, sem_p,
+):
+    n = lax.axis_size("ea")
+    me, here = lax.axis_index("ea"), lax.axis_index("sa")
+    partner = here + 1 - 2 * lax.rem(here, 2)
+    half = weight_ref.shape[0] // 2
+    mine = pl.ds(pl.multiple_of(lax.rem(here, 2) * half, half), half)
+    exp_dev, tokens, width = down_hbm.shape[0], res_ref.shape[0], res_ref.shape[1]
+    top = named_ref.shape[0] // 2
+    tile = 512
+    tiles = width // tile
+
+    def peer(d):
+        return lax.rem(me + d, n)
+
+    def origin(d):
+        return lax.rem(me + n - d, n)
+
+    def remote(src, dst, sems, d, where):
+        return pltpu.make_async_remote_copy(
+            src_ref=src, dst_ref=dst, send_sem=sems.at[0, d], recv_sem=sems.at[1, d],
+            device_id=where, device_id_type=MESH,
+        )
+
+    def table_copy(d):
+        return remote(named_ref, table_ref.at[me], sem_t, d, {"ea": peer(d)})
+
+    def weight_copy(d):
+        return remote(weight_ref.at[mine], full_ref.at[me, mine], sem_w, d, {"ea": peer(d)})
+
+    def forward_copy(d):
+        block = full_ref.at[origin(d), mine]
+        return remote(block, block, sem_f, d, {"sa": partner})
+
+    def partial_copy(d):
+        return remote(send_ref.at[peer(d)], got_ref.at[d], sem_p, d, {"ea": peer(d)})
+
+    def each(action):
+        def turn(d, carry):
+            action(d)
+            return carry
+
+        lax.fori_loop(1, n, turn, 0)
+
+    loads = []
+    for e in range(exp_dev):
+        loads.append((
+            pltpu.make_async_copy(hidden_hbm.at[e], hidden_ref.at[e], load_sem.at[0, e]),
+            pltpu.make_async_copy(down_hbm.at[e], down_ref.at[e], load_sem.at[1, e]),
+        ))
+        for copy in loads[-1]:
+            copy.start()
+    own = pltpu.make_async_copy(weight_ref, full_ref.at[me], own_sem)
+    own.start()
+
+    barrier = pltpu.get_barrier_semaphore()
+    each(lambda d: pl.semaphore_signal(barrier, inc=1, device_id={"ea": peer(d)}, device_id_type=MESH))
+    pl.semaphore_signal(barrier, inc=1, device_id={"sa": partner}, device_id_type=MESH)
+    pl.semaphore_wait(barrier, n)
+
+    each(lambda d: table_copy(d).start())
+    each(lambda d: weight_copy(d).start())
+
+    for e in range(exp_dev):
+        for copy in loads[e]:
+            copy.wait()
+        if pad > cap:
+            made_ref[:, e * pad + cap : (e + 1) * pad, :] = jnp.zeros((n, pad - cap, width), BF16)
+
+        def project(t, carry):
+            cols = pl.ds(pl.multiple_of(t * tile, tile), tile)
+            made = jnp.dot(hidden_ref[e], down_ref[e, :, cols], preferred_element_type=F32)
+            for s in range(n):
+                made_ref[s, e * pad : e * pad + cap, cols] = made[s * cap : (s + 1) * cap].astype(BF16)
+            return carry
+
+        lax.fori_loop(0, tiles, project, 0)
+
+    table_ref[me] = named_ref[...]
+    row, col = iotas(tokens, tokens)
+    after = (row < col).astype(BF16)
+    place = lax.broadcasted_iota(jnp.int32, (pad, tokens), 0).astype(F32)
+
+    def partial(d, carry):
+        s = peer(d)
+
+        @pl.when(d < n)
+        def _():
+            table_copy(n - d).wait_recv()
+
+        named = table_ref[s]
+        ids, weights = named[:top], named[top:]
+        parts = []
+        for e in range(exp_dev):
+            hit = ids == (me * exp_dev + e).astype(F32)
+            count = jnp.sum(hit.astype(F32), axis=0, keepdims=True)
+            weight = jnp.sum(jnp.where(hit, weights, 0.0), axis=0, keepdims=True)
+            slot = jnp.dot(
+                jnp.broadcast_to(count, (pad, tokens)).astype(BF16), after, preferred_element_type=F32
+            )
+            parts.append(jnp.where((slot == place) & (count > 0.0), weight, 0.0))
+        mix_ref[...] = jnp.concatenate(parts, axis=0).T.astype(BF16)
+
+        def block(t, inner):
+            cols = pl.ds(pl.multiple_of(t * tile, tile), tile)
+            send_ref[s, :, cols] = jnp.dot(
+                mix_ref[...], made_ref[s, :, cols], preferred_element_type=F32
+            ).astype(BF16)
+            return inner
+
+        lax.fori_loop(0, tiles, block, 0)
+
+        @pl.when(d < n)
+        def _():
+            partial_copy(d).start()
+
+        return carry
+
+    lax.fori_loop(1, n + 1, partial, 0)
+
+    sum_decays(decay_ref, decay_t_ref, sum_ref, sum_t_ref)
+
+    def maps(kh, carry):
+        cols = pl.ds(pl.multiple_of(kh * DK, DK), DK)
+        outs = key_head_maps(kh, q_ref[:, cols], k_ref[:, cols], rate_ref, rate_t_ref, sum_ref, sum_t_ref)
+        for u, (mn, ga) in enumerate(outs):
+            mn_ref[kh * (HV // HK) + u] = mn
+            ga_ref[kh * (HV // HK) + u] = ga
+        return carry
+
+    lax.fori_loop(0, HK, maps, 0)
+
+    def pass_on(d):
+        weight_copy(d).wait_recv()
+        forward_copy(d).start()
+
+    each(pass_on)
+    each(lambda d: partial_copy(d).wait_recv())
+
+    def close(r, carry):
+        rows = pl.ds(pl.multiple_of(r * 16, 16), 16)
+        moe = send_ref[me, rows, :].astype(F32)
+        for d in range(1, n):
+            moe = moe + got_ref[d, rows, :].astype(F32)
+        stream = (res_ref[rows, :].astype(F32) + moe).astype(BF16).astype(F32)
+        scale = lax.rsqrt(jnp.mean(stream * stream, axis=-1, keepdims=True) + 1e-06)
+        normed_ref[rows, :] = (stream * scale * gain_ref[...].astype(F32)).astype(BF16)
+        return carry
+
+    lax.fori_loop(0, tokens // 16, close, 0)
+    own.wait()
+
+    def finish(d):
+        forward_copy(d).wait()
+        table_copy(d).wait_send()
+        weight_copy(d).wait_send()
+        partial_copy(d).wait_send()
+
+    each(finish)
+
+
+def gather_stage(n, named, hidden, down, residual, gain, weight, queries, keys, decay, rate):
+    exp_dev, rows, ff_units = hidden.shape
+    tokens, width = residual.shape
+    cap = rows // n
+    pad = -(-cap // 16) * 16
+    vmem = pl.BlockSpec(memory_space=pltpu.VMEM)
+    hbm = pl.BlockSpec(memory_space=pl.ANY)
+    maps = jax.ShapeDtypeStruct((HV, tokens + DK, DK), BF16)
+    dma = pltpu.SemaphoreType.DMA
+    return pl.pallas_call(
+        functools.partial(gather_kernel, cap, pad),
+        out_shape=(
+            jax.ShapeDtypeStruct((tokens, width), BF16),
+            jax.ShapeDtypeStruct((n,) + weight.shape, BF16),
+            maps,
+            maps,
+        ),
+        in_specs=[vmem, hbm, hbm] + [vmem] * 9,
+        out_specs=[vmem, hbm, vmem, vmem],
+        scratch_shapes=[
+            pltpu.VMEM((n,) + named.shape, F32),
+            pltpu.VMEM(hidden.shape, BF16),
+            pltpu.VMEM(down.shape, BF16),
+            pltpu.VMEM((n, exp_dev * pad, width), BF16),
+            pltpu.VMEM((tokens, exp_dev * pad), BF16),
+            pltpu.VMEM((n, tokens, width), BF16),
+            pltpu.VMEM((n, tokens, width), BF16),
+            pltpu.VMEM((tokens, HV), F32),
+            pltpu.VMEM((HV, tokens), F32),
+            dma((2, exp_dev)),
+            dma,
+            dma((2, n)),
+            dma((2, n)),
+            dma((2, n)),
+            dma((2, n)),
+        ],
+        compiler_params=pltpu.CompilerParams(
+            vmem_limit_bytes=VMEM_BYTES, collective_id=0, has_side_effects=True
+        ),
+        name="gather",
+    )(named, hidden, down, residual, gain.reshape(1, width), weight, queries, keys, decay, decay.T, rate, rate.T)
+
+
+def chain_kernel(normed_ref, weight_ref, mn_ref, ga_ref, out_ref, send_ref, got_ref, sem):
+    g, groups = pl.program_id(0), pl.num_programs(0)
+    n, here = lax.axis_size("sa"), lax.axis_index("sa")
+    tokens = normed_ref.shape[0]
+    per = mn_ref.shape[0]
+    following, previous = lax.rem(here + 1, n), lax.rem(here + n - 1, n)
+
+    @pl.when(g == 0)
+    def _():
+        barrier = pltpu.get_barrier_semaphore()
+        for where in (following, previous):
+            pl.semaphore_signal(barrier, inc=1, device_id={"sa": where}, device_id_type=MESH)
+        pl.semaphore_wait(barrier, 2)
+        got_ref_first = jnp.zeros(got_ref.shape[1:], BF16)
+
+        @pl.when(here == 0)
+        def _():
+            for i in range(got_ref.shape[0]):
+                got_ref[i] = got_ref_first
+
+    def copy(i):
+        return pltpu.make_async_remote_copy(
+            src_ref=send_ref.at[i], dst_ref=got_ref.at[i], send_sem=sem.at[0, i],
+            recv_sem=sem.at[1, i], device_id={"sa": following}, device_id_type=MESH,
+        )
+
+    values = jnp.dot(normed_ref[...], weight_ref[...], preferred_element_type=F32).astype(BF16)
+    both = [
+        jnp.dot(mn_ref[u], values[:, u * DV : (u + 1) * DV], preferred_element_type=F32)
+        for u in range(per)
+    ]
+
+    @pl.when(here > 0)
+    def _():
+        copy(g).wait_recv()
+
+    after = [
+        both[u] + jnp.dot(ga_ref[u], got_ref[g, u], preferred_element_type=F32) for u in range(per)
+    ]
+    for u in range(per):
+        send_ref[g, u] = after[u][tokens:].astype(BF16)
+
+    @pl.when(here < n - 1)
+    def _():
+        copy(g).start()
+
+    for u in range(per):
+        out_ref[:, u * DV : (u + 1) * DV] = after[u][:tokens].astype(BF16)
+
+    @pl.when((g == groups - 1) & (here < n - 1))
+    def _():
+        for i in range(send_ref.shape[0]):
+            copy(i).wait_send()
+
+
+def chain_stage(normed, weight, mn, ga):
+    tokens, width = normed.shape
+    per = 4
+    groups = HV // per
+    tile = per * DV
+    states = pltpu.VMEM((groups, per, DK, DV), BF16)
+    maps = pl.BlockSpec((per, tokens + DK, DK), lambda g: (g, 0, 0))
+    return pl.pallas_call(
+        chain_kernel,
+        grid=(groups,),
+        out_shape=jax.ShapeDtypeStruct((tokens, HV * DV), BF16),
+        in_specs=[
+            pl.BlockSpec((tokens, width), lambda g: (0, 0)),
+            pl.BlockSpec((width, tile), lambda g: (0, g)),
+            maps,
+            maps,
+        ],
+        out_specs=pl.BlockSpec((tokens, tile), lambda g: (0, g)),
+        scratch_shapes=[states, states, pltpu.SemaphoreType.DMA((2, groups))],
+        compiler_params=pltpu.CompilerParams(
+            vmem_limit_bytes=VMEM_BYTES, collective_id=1, has_side_effects=True
+        ),
+        name="chain",
+    )(normed, weight, mn, ga)
 
 
 def on_device(
@@ -313,11 +620,18 @@
     exp_dev, rows, ff_units = expert_hidden.shape
     cap = rows // n_ea
     tokens = residual.shape[1]
+    named = jnp.concatenate([expert_ids[0].astype(F32), combine_weight[0]], axis=-1)
+    fits = n_ea * tokens * residual.shape[2] <= 4 * 1024 * 1024 and cap % 8 == 0
+    if fits and lax.axis_size("sa") % 2 == 0:
+        normed, weight, mn, ga = gather_stage(
+            n_ea, named.T, expert_hidden, down_weight, residual[0], norm_gain, value_weight,
+            queries[0], keys[0], log_decay[0], write_rate[0],
+        )
+        return chain_stage(normed, weight.reshape(-1, weight.shape[2]), mn, ga)[None]
     pad = -(-cap // 16) * 16
     hidden = jnp.pad(
         expert_hidden.reshape(exp_dev, n_ea, cap, ff_units), ((0, 0), (0, 0), (0, pad - cap), (0, 0))
     ).reshape(exp_dev, n_ea * pad, ff_units)
-    named = jnp.concatenate([expert_ids[0].astype(F32), combine_weight[0]], axis=-1)
     named = lax.all_gather(named, "ea")
     weight = lax.all_gather(value_weight, "ea", axis=0, tiled=True)
     partial = expert_partials(hidden, down_weight, named, n_ea, tokens)

time: 337 us -> 216 us (0.64)
  waiting for transfers between devices: 233 us -> 0 us
  Pallas kernels: 57.3 us -> 207 us
  blocking collectives: 21.8 us -> 0 us
  between operations: 13.1 us -> 0.02 us
    all_gather x3 -> x0, waiting for transfers between devices: 165 us -> none  [the longest x1 123 us: on_device(): weight = lax.all_gather(value_weight, 'ea', axis=0, tiled=True)]
    pallas_call x4 -> x2, Pallas kernels: 57.3 us -> 207 us  [the longest x1 191 us: gather_stage(): pl.pallas_call(functools.partial(gather_kernel, cap, pad), out_shape=(jax...]
    reduce_scatter x1 -> x0, waiting for transfers between devices: 66.6 us -> none  [on_device(): moe = lax.psum_scatter(partial, 'ea', scatter_dimension=0, tiled=True)[0]]
    all_gather x1 -> x0, blocking collectives: 21.8 us -> none  [on_device(): named = lax.all_gather(named, 'ea')]
  transfers between devices with their start and end apart: 4 -> 0, of which waited for: 4 -> 0; matrix products, arithmetic and copies ran while one was open for 1% -> 0% of each run, Pallas kernels for 10% -> 0%
where the time goes in v2:
time: 216 us; the launch traced here: 215 us
  Pallas kernels  207 us (96%)
  local copies, waits for them, and re-layouts  6.7 us (3%)
    pallas_call x1, Pallas kernels, gather_stage(): pl.pallas_call(functools.partial(gather_kernel, cap, pad), out_shape=(jax...  191 us
    pallas_call x1, Pallas kernels, chain_stage(): pl.pallas_call(chain_kernel, grid=(groups,), out_shape=jax.ShapeDtypeStru...  15.9 us

profile of v2, /device:TPU:15, one launch (start us, length us, event | category | flops | bytes accessed | tf_op | source)
XLA Modules:
  0.0 215.4 jit_solution(2387299841771868395)
XLA Ops:
  0.0 0.7 fusion
  0.7 0.7 copy.20
  1.4 0.6 maximum_bitcast_fusion.named_ref
  2.0 1.3 reshape.7.gain_ref
  3.3 1.4 copy.14.rate_ref
  4.7 1.4 copy.13.decay_ref
  6.1 191.4 %gather.1 = (bf16[128,2048]{1,0:T(8,128)(2,1)}, bf16[8,256,2048]{2,1,0:T(8,128)(2,1)}, bf16[16,256,128]{2,1,0:T(8,128)(2,1)}, bf16[16,256,128]{2,1,0:T(8,128)(2,1)}) custom-call(f32[20,128]{1,0:T(8,128)} %maximum_bitcast_fusion.named_ref, bf16[4,448,512]{2,1,0:T(8,128)(2,1)} %hidden_hbm.1, bf16[4,512,2048]{2,1,0:T(8,128)(2,1)} %down_hbm.1, ...), custom_call_target="tpu_custom_call" | custom-call | tf_op jit(solution)/shard_map/gather/pallas_call | solution.py:491
  197.6 15.9 %chain.1 = bf16[128,2048]{1,0:T(8,128)(2,1)} custom-call(bf16[128,2048]{1,0:T(8,128)(2,1)} %get-tuple-element.9.normed_ref, bf16[2048,2048]{1,0:T(8,128)(2,1)} %bitcast.18, bf16[16,256,128]{2,1,0:T(8,128)(2,1)} %get-tuple-element.11.mn_ref, bf16[16,256,128]{2,1,0:T(8,128)(2,1)} %get-tuple-element.12.ga_ref), custom_call_target="tpu_custom_call" | custom-call | tf_op jit(solution)/shard_map/chain/pallas_call | solution.py:587
  213.5 1.9 copy.22

commit v3 on v2

--- a/solution.py
+++ b/solution.py
@@ -317,14 +317,18 @@
     named_ref, hidden_hbm, down_hbm, res_ref, gain_ref, weight_ref, q_ref, k_ref,
     decay_ref, decay_t_ref, rate_ref, rate_t_ref,
     normed_ref, full_ref, mn_ref, ga_ref,
-    table_ref, hidden_ref, down_ref, made_ref, mix_ref, send_ref, got_ref, sum_ref, sum_t_ref,
-    load_sem, own_sem, sem_t, sem_w, sem_f, sem_p,
+    table_ref, hidden_ref, down_ref, made_ref, mix_ref, send_ref, got_ref, mate_ref, sum_ref, sum_t_ref,
+    load_sem, own_sem, sem_t, sem_w, sem_f, sem_y, sem_g, sem_m, sem_p,
 ):
     n = lax.axis_size("ea")
     me, here = lax.axis_index("ea"), lax.axis_index("sa")
     partner = here + 1 - 2 * lax.rem(here, 2)
-    half = weight_ref.shape[0] // 2
-    mine = pl.ds(pl.multiple_of(lax.rem(here, 2) * half, half), half)
+    across = lax.rem(here + 2, 4)
+    part = weight_ref.shape[0] // 4
+    mine = pl.ds(pl.multiple_of(here * part, part), part)
+    others = pl.ds(pl.multiple_of(across * part, part), part)
+    lines, line, side = n // 2, me // 2, lax.rem(me, 2)
+    mate = line * 2 + 1 - side
     exp_dev, tokens, width = down_hbm.shape[0], res_ref.shape[0], res_ref.shape[1]
     top = named_ref.shape[0] // 2
     tile = 512
@@ -352,8 +356,23 @@
         block = full_ref.at[origin(d), mine]
         return remote(block, block, sem_f, d, {"sa": partner})
 
-    def partial_copy(d):
-        return remote(send_ref.at[peer(d)], got_ref.at[d], sem_p, d, {"ea": peer(d)})
+    def across_copy(d):
+        block = full_ref.at[origin(d), mine]
+        return remote(block, block, sem_y, d, {"sa": across})
+
+    def second_copy(d):
+        block = full_ref.at[origin(d), others]
+        return remote(block, block, sem_g, d, {"sa": partner})
+
+    def beyond(i):
+        return lax.rem(line + 1 + i, lines) * 2
+
+    def mate_copy(i):
+        return remote(send_ref.at[beyond(i) + 1 - side], mate_ref.at[i], sem_m, i, {"ea": mate})
+
+    def partial_copy(i):
+        there = beyond(i) + side
+        return remote(send_ref.at[there], got_ref.at[i], sem_p, i, {"ea": there})
 
     def each(action):
         def turn(d, carry):
@@ -376,7 +395,8 @@
     barrier = pltpu.get_barrier_semaphore()
     each(lambda d: pl.semaphore_signal(barrier, inc=1, device_id={"ea": peer(d)}, device_id_type=MESH))
     pl.semaphore_signal(barrier, inc=1, device_id={"sa": partner}, device_id_type=MESH)
-    pl.semaphore_wait(barrier, n)
+    pl.semaphore_signal(barrier, inc=1, device_id={"sa": across}, device_id_type=MESH)
+    pl.semaphore_wait(barrier, n + 1)
 
     each(lambda d: table_copy(d).start())
     each(lambda d: weight_copy(d).start())
@@ -401,13 +421,9 @@
     after = (row < col).astype(BF16)
     place = lax.broadcasted_iota(jnp.int32, (pad, tokens), 0).astype(F32)
 
-    def partial(d, carry):
-        s = peer(d)
-
-        @pl.when(d < n)
-        def _():
-            table_copy(n - d).wait_recv()
-
+    each(lambda d: table_copy(d).wait_recv())
+
+    def mixing(s):
         named = table_ref[s]
         ids, weights = named[:top], named[top:]
         parts = []
@@ -421,22 +437,30 @@
             parts.append(jnp.where((slot == place) & (count > 0.0), weight, 0.0))
         mix_ref[...] = jnp.concatenate(parts, axis=0).T.astype(BF16)
 
+    def combine(s, extra):
+        mixing(s)
+
         def block(t, inner):
             cols = pl.ds(pl.multiple_of(t * tile, tile), tile)
-            send_ref[s, :, cols] = jnp.dot(
-                mix_ref[...], made_ref[s, :, cols], preferred_element_type=F32
-            ).astype(BF16)
+            total = jnp.dot(mix_ref[...], made_ref[s, :, cols], preferred_element_type=F32)
+            if extra is not None:
+                total = total + mate_ref[extra, :, cols].astype(F32)
+            send_ref[s, :, cols] = total.astype(BF16)
             return inner
 
         lax.fori_loop(0, tiles, block, 0)
 
-        @pl.when(d < n)
-        def _():
-            partial_copy(d).start()
-
+    def to_mate(i, carry):
+        combine(beyond(i) + 1 - side, None)
+        mate_copy(i).start()
         return carry
 
-    lax.fori_loop(1, n + 1, partial, 0)
+    lax.fori_loop(0, lines, to_mate, 0)
+
+    def pass_on(d):
+        weight_copy(d).wait_recv()
+        across_copy(d).start()
+        forward_copy(d).start()
 
     sum_decays(decay_ref, decay_t_ref, sum_ref, sum_t_ref)
 
@@ -446,21 +470,41 @@
         for u, (mn, ga) in enumerate(outs):
             mn_ref[kh * (HV // HK) + u] = mn
             ga_ref[kh * (HV // HK) + u] = ga
+
+        @pl.when(kh + 1 < n)
+        def _():
+            pass_on(kh + 1)
+
         return carry
 
     lax.fori_loop(0, HK, maps, 0)
-
-    def pass_on(d):
-        weight_copy(d).wait_recv()
-        forward_copy(d).start()
-
-    each(pass_on)
-    each(lambda d: partial_copy(d).wait_recv())
+    for d in range(HK + 1, n):
+        pass_on(d)
+
+    def along(i, carry):
+        mate_copy(i).wait_recv()
+        combine(beyond(i) + side, i)
+
+        @pl.when(i < lines - 1)
+        def _():
+            partial_copy(i).start()
+
+        return carry
+
+    lax.fori_loop(0, lines, along, 0)
+
+    def pass_second(d):
+        across_copy(d).wait_recv()
+        second_copy(d).start()
+
+    each(pass_second)
+    for i in range(lines - 1):
+        partial_copy(i).wait_recv()
 
     def close(r, carry):
         rows = pl.ds(pl.multiple_of(r * 16, 16), 16)
         moe = send_ref[me, rows, :].astype(F32)
-        for d in range(1, n):
+        for d in range(lines - 1):
             moe = moe + got_ref[d, rows, :].astype(F32)
         stream = (res_ref[rows, :].astype(F32) + moe).astype(BF16).astype(F32)
         scale = lax.rsqrt(jnp.mean(stream * stream, axis=-1, keepdims=True) + 1e-06)
@@ -474,9 +518,14 @@
         forward_copy(d).wait()
         table_copy(d).wait_send()
         weight_copy(d).wait_send()
-        partial_copy(d).wait_send()
+        across_copy(d).wait_send()
+        second_copy(d).wait()
 
     each(finish)
+    for i in range(lines):
+        mate_copy(i).wait_send()
+        if i < lines - 1:
+            partial_copy(i).wait_send()
 
 
 def gather_stage(n, named, hidden, down, residual, gain, weight, queries, keys, decay, rate):
@@ -505,7 +554,8 @@
             pltpu.VMEM((n, exp_dev * pad, width), BF16),
             pltpu.VMEM((tokens, exp_dev * pad), BF16),
             pltpu.VMEM((n, tokens, width), BF16),
-            pltpu.VMEM((n, tokens, width), BF16),
+            pltpu.VMEM((max(n // 2 - 1, 1), tokens, width), BF16),
+            pltpu.VMEM((n // 2, tokens, width), BF16),
             pltpu.VMEM((tokens, HV), F32),
             pltpu.VMEM((HV, tokens), F32),
             dma((2, exp_dev)),
@@ -514,6 +564,9 @@
             dma((2, n)),
             dma((2, n)),
             dma((2, n)),
+            dma((2, n)),
+            dma((2, n // 2)),
+            dma((2, n // 2)),
         ],
         compiler_params=pltpu.CompilerParams(
             vmem_limit_bytes=VMEM_BYTES, collective_id=0, has_side_effects=True
@@ -622,7 +675,7 @@
     tokens = residual.shape[1]
     named = jnp.concatenate([expert_ids[0].astype(F32), combine_weight[0]], axis=-1)
     fits = n_ea * tokens * residual.shape[2] <= 4 * 1024 * 1024 and cap % 8 == 0
-    if fits and lax.axis_size("sa") % 2 == 0:
+    if fits and n_ea % 2 == 0 and lax.axis_size("sa") == 4:
         normed, weight, mn, ga = gather_stage(
             n_ea, named.T, expert_hidden, down_weight, residual[0], norm_gain, value_weight,
             queries[0], keys[0], log_decay[0], write_rate[0],

time: 216 us -> 133 us (0.62)
  Pallas kernels: 207 us -> 123 us
    pallas_call x1, Pallas kernels: 191 us -> 107 us  [gather_stage(): pl.pallas_call(functools.partial(gather_kernel, cap, pad), out_shape=(jax...]
where the time goes in v3:
time: 133 us; the launch traced here: 131 us
  Pallas kernels  123 us (92%)
  local copies, waits for them, and re-layouts  6.7 us (5%)
    pallas_call x1, Pallas kernels, gather_stage(): pl.pallas_call(functools.partial(gather_kernel, cap, pad), out_shape=(jax...  107 us
    pallas_call x1, Pallas kernels, chain_stage(): pl.pallas_call(chain_kernel, grid=(groups,), out_shape=jax.ShapeDtypeStru...  16.8 us

profile of v3, /device:TPU:15, one launch (start us, length us, event | category | flops | bytes accessed | tf_op | source)
XLA Modules:
  0.0 131.5 jit_solution(10076230082597790472)
XLA Ops:
  0.0 0.7 fusion
  0.7 0.7 copy.20
  1.4 0.6 maximum_bitcast_fusion.named_ref
  2.0 1.3 reshape.7.gain_ref
  3.3 1.4 %copy.14.rate_ref = f32[128,16]{1,0:T(8,128)} copy(f32[128,16]{0,1:T(8,128)} %bitcast.26) | data formatting | bytes 16384 | tf_op jit(solution)/shard_map/squeeze | solution.py:681
  4.7 1.4 %copy.13.decay_ref = f32[128,16]{1,0:T(8,128)} copy(f32[128,16]{0,1:T(8,128)} %bitcast.24) | data formatting | bytes 16384 | tf_op jit(solution)/shard_map/squeeze | solution.py:681
  6.1 106.7 %gather.1 = (bf16[128,2048]{1,0:T(8,128)(2,1)}, bf16[8,256,2048]{2,1,0:T(8,128)(2,1)}, bf16[16,256,128]{2,1,0:T(8,128)(2,1)}, bf16[16,256,128]{2,1,0:T(8,128)(2,1)}) custom-call(f32[20,128]{1,0:T(8,128)} %maximum_bitcast_fusion.named_ref, bf16[4,448,512]{2,1,0:T(8,128)(2,1)} %hidden_hbm.1, bf16[4,512,2048]{2,1,0:T(8,128)(2,1)} %down_hbm.1, ...), custom_call_target="tpu_custom_call" | custom-call | tf_op jit(solution)/shard_map/gather/pallas_call | solution.py:540
  112.8 16.8 %chain.1 = bf16[128,2048]{1,0:T(8,128)(2,1)} custom-call(bf16[128,2048]{1,0:T(8,128)(2,1)} %get-tuple-element.9.normed_ref, bf16[2048,2048]{1,0:T(8,128)(2,1)} %bitcast.18, bf16[16,256,128]{2,1,0:T(8,128)(2,1)} %get-tuple-element.11.mn_ref, bf16[16,256,128]{2,1,0:T(8,128)(2,1)} %get-tuple-element.12.ga_ref), custom_call_target="tpu_custom_call" | custom-call | tf_op jit(solution)/shard_map/chain/pallas_call | solution.py:640
  129.6 1.9 %copy.22 = bf16[1,128,2048]{2,1,0:T(8,128)(2,1)} copy(bf16[1,128,2048]{2,1,0:T(8,128)(2,1)} %bitcast.19) | data formatting | bytes 1048576
